TPU v7x, 512 devices: a whole 4x4x16 slice. The times are simulated.
512 devices in a mesh: depth: 32 (over x, y, core), area: 16 (over z).
Axes of the slice: x: 4, y: 4, z: 16, core: 2. Of those that a mesh axis runs over, the one named last changes fastest.
Arguments:
- rhs_field: float32 [64, 32, 8192], P('depth', None, 'area'), may hold values from -8 to 8
- start_field: float32 [64, 32, 8192], P('depth', None, 'area'), may hold values from -4 to 4
- inverses: float32 [64, 8192, 512], P('depth', 'area'), may hold values from -0.044194174 to 1
- facies: int32 [64, 8192], P('depth', 'area'), may hold values from 0 to 7
- neighbours: int32 [8192, 4], P('area'), may hold values from 0 to 639, as said below
- lateral_table: float32 [8, 4], replicated, may hold values from 0.05 to 0.3
- vertical_table: float32 [8], replicated, may hold values from 0.9 to 1
Outputs:
- updated: float32 [64, 32, 8192], P('depth', None, 'area')
Inputs may be any that keep to these rules, and one draw needn't show every extreme that they name: `neighbours`: index 64 + c is column c itself; entries 0 and 1 of column c are c - 1 and c + 1, the others lie within 64 columns of c and differ from it.
All inputs are finite; a program needn't handle non-finite values.
Results may differ from a plain program's by a relative error of at most 0.00016.
Values sent between devices are 32-bit elements; how exact they have to be, the bound alone decides.
A program may use at most 128 MiB of HBM per device.

v0:
```python
import functools

import jax
import jax.numpy as jnp
from jax import lax
from jax.experimental import pallas as pl
from jax.experimental.pallas import tpu as pltpu
from jax.sharding import PartitionSpec as P

MESH = pl.DeviceIdType.MESH
F32 = jnp.float32
BF16 = jnp.bfloat16
HW = 64
LANES = 128
ROW = 8
HUB = ROW - 1
BLOCKS = 8

SENDS = (
    "start_right", "start_left", "below", "f_next", "down_hub", "down6",
    "down5", "down3", "down1", "down_pair", "y_right", "y_left",
    "w_pair", "w_hub", "g_prev", "up_hub", "up6", "up5",
    "up3", "up1", "up_pair",
)
RECVS = (
    "start_lo", "start_hi", "below", "f", "down", "y_lo",
    "y_hi", "w_pair", "w0", "w1", "w2", "g",
    "up",
)


def split(x):
    high = x.astype(BF16)
    return high, (x - high.astype(F32)).astype(BF16)


def dot3(x, w_high, w_low, transposed=False):
    high, low = split(x)
    dims = (((1,), (1 if transposed else 0,)), ((), ()))
    rows = x.shape[0]
    both = lax.dot_general(
        jnp.concatenate([high, low], axis=0), w_high, dims, preferred_element_type=F32
    )
    rest = lax.dot_general(high, w_low, dims, preferred_element_type=F32)
    return both[:rows] + both[rows:] + rest


def kernel(
    depth, areas,
    lat_tab, vert_tab, facies, nbrs, rhs_hbm, start_hbm, inv_hbm,
    out,
    rhs, start, inv, dh, dl, th, tl, ina, ah, al, outa, ins, sh, sl, outs, mh, ml,
    lat_h, lat_l, wts, wsum, vert, slo, shi, ylo, yhi, below_out, below_in,
    g, f_in, f_out, o_buf, eb, e_next, e_in, y, h, p_buf, w_out, w_pair, w_hub, o_up,
    g_in, g_out, ub, u_next,
    local, snd, rcv, snd_a, rcv_a, snd_s, rcv_s,
):
    rows = depth // ROW
    d = lax.axis_index("depth")
    z = lax.axis_index("area")
    r, c = d // ROW, d % ROW
    width = out.shape[2]
    count = out.shape[1]
    tiles = width // LANES
    size = width // BLOCKS
    base = r * ROW
    waits = []

    def both(*conds):
        return functools.reduce(jnp.logical_and, conds)

    def copy(src, dst, send, recv, depth_id, area_id=None):
        return pltpu.make_async_remote_copy(
            src_ref=src,
            dst_ref=dst,
            send_sem=snd.at[SENDS.index(send)],
            recv_sem=rcv.at[RECVS.index(recv)],
            device_id=(depth_id, z if area_id is None else area_id),
            device_id_type=MESH,
        )

    def send(cond, args):
        waits.append((cond, args))
        copy(*args()).start()

    def received(dst, recv):
        copy(dst, dst, SENDS[0], recv, d).wait_recv()

    def block_a(b):
        return pltpu.make_async_remote_copy(
            src_ref=outa.at[b], dst_ref=ina.at[b], send_sem=snd_a.at[b], recv_sem=rcv_a.at[b],
            device_id=(d + 1, z), device_id_type=MESH,
        )

    def block_s(b):
        return pltpu.make_async_remote_copy(
            src_ref=outs.at[b], dst_ref=ins.at[b], send_sem=snd_s.at[b], recv_sem=rcv_s.at[b],
            device_id=(d - 1, z), device_id_type=MESH,
        )

    loads = [
        pltpu.make_async_copy(start_hbm, start, local.at[0]),
        pltpu.make_async_copy(inv_hbm.at[1], inv.at[1], local.at[1]),
        pltpu.make_async_copy(inv_hbm.at[0], inv.at[0], local.at[2]),
        pltpu.make_async_copy(rhs_hbm, rhs, local.at[3]),
    ]
    for load in loads:
        load.start()

    barrier = pltpu.get_barrier_semaphore()
    is_spoke = both(c % 2 == 1, c < HUB)
    partners = [
        (d > 0, d - 1, z),
        (d < depth - 1, d + 1, z),
        (z > 0, d, z - 1),
        (z < areas - 1, d, z + 1),
        (is_spoke, base + HUB, z),
        (both(c == HUB, r > 0), d - ROW, z),
        (both(c == HUB, r < rows - 1), d + ROW, z),
    ] + [(c == HUB, base + spoke, z) for spoke in (1, 3, 5)]
    for cond, to_depth, to_area in partners:

        @pl.when(cond)
        def _():
            pl.semaphore_signal(
                barrier, inc=1, device_id=(to_depth, to_area), device_id_type=MESH
            )

    kinds = facies[...]
    facies_count = lat_tab.shape[1]
    v_rows = jnp.zeros(kinds.shape, F32)
    w_rows = [jnp.zeros(kinds.shape, F32) for _ in range(lat_tab.shape[0])]
    for kind in range(facies_count):
        mask = kinds == kind
        v_rows = jnp.where(mask, vert_tab[kind], v_rows)
        w_rows = [jnp.where(mask, lat_tab[j, kind], w) for j, w in enumerate(w_rows)]
    vert[...] = v_rows
    for j, w in enumerate(w_rows):
        wts[j] = w
    wsum[...] = functools.reduce(jnp.add, w_rows)

    for t in range(tiles):
        lanes = slice(t * LANES, (t + 1) * LANES)
        for k in range(2):
            for first in (0, 2 * LANES + HW):
                lat_h[k, t, first : first + HW, :] = jnp.zeros((HW, LANES), BF16)
                lat_l[k, t, first : first + HW, :] = jnp.zeros((HW, LANES), BF16)
        for first in range(HW, 2 * LANES + HW, HW):
            place = lax.broadcasted_iota(jnp.int32, (HW, LANES), 0) + (first + t * LANES - HW)
            sums = [jnp.zeros((HW, LANES), F32) for _ in range(2)]
            for j in range(nbrs.shape[0]):
                hit = place == nbrs[j : j + 1, lanes]
                for k in range(2):
                    sums[k] = sums[k] + jnp.where(hit, wts[j, k : k + 1, lanes], 0.0)
            for k in range(2):
                high, low = split(sums[k])
                lat_h[k, t, first : first + HW, :] = high
                lat_l[k, t, first : first + HW, :] = low

    def lateral(k, v, low, high):
        parts = [low[k]] + [v[:, t * LANES : (t + 1) * LANES] for t in range(tiles)] + [high[k]]
        sums = [
            dot3(jnp.concatenate(parts[t : t + 3], axis=1), lat_h[k, t], lat_l[k, t])
            for t in range(tiles)
        ]
        return wsum[k : k + 1, :] * v - jnp.concatenate(sums, axis=1)

    loads[0].wait()
    below_out[...] = vert[0:1, :] * start[0]
    partner_count = sum(cond.astype(jnp.int32) for cond, _, _ in partners)
    pl.semaphore_wait(barrier, partner_count)

    has_left, has_right = z > 0, z < areas - 1

    def halo(field, low, high, name):
        @pl.when(has_right)
        def _():
            send(lambda: has_right, lambda: (
                field.at[:, :, pl.ds(width - LANES, LANES)], low,
                name + "_right", name + "_lo", d, z + 1,
            ))

        @pl.when(has_left)
        def _():
            send(lambda: has_left, lambda: (
                field.at[:, :, pl.ds(0, LANES)], high,
                name + "_left", name + "_hi", d, z - 1,
            ))

        @pl.when(jnp.logical_not(has_left))
        def _():
            low[...] = jnp.zeros(low.shape, F32)

        @pl.when(jnp.logical_not(has_right))
        def _():
            high[...] = jnp.zeros(high.shape, F32)

    def halo_received(low, high, name):
        @pl.when(has_left)
        def _():
            received(low, name + "_lo")

        @pl.when(has_right)
        def _():
            received(high, name + "_hi")

    halo(start, slo, shi, "start")

    @pl.when(d > 0)
    def _():
        send(lambda: d > 0, lambda: (below_out, below_in, "below", "below", d - 1))

    def split_layer(k):
        def body(i, _):
            some = pl.ds(pl.multiple_of(i * LANES, LANES), LANES)
            high, low = split(inv[k, some, :])
            dh[k, some, :] = high
            dl[k, some, :] = low
            return 0

        lax.fori_loop(0, tiles, body, 0)

    per_tile = LANES // size
    loads[1].wait()
    split_layer(1)
    loads[2].wait()

    def compose(i, _):
        some = pl.ds(pl.multiple_of(i * LANES, LANES), LANES)
        scale = jnp.transpose(jnp.broadcast_to(vert[0:1, some], (LANES, LANES)))
        left = inv[0, some, :] * vert[1:2, :] * jnp.concatenate([scale] * tiles, axis=1)
        product = dot3(left, dh[1], dl[1])
        high, low = split(product)
        th[some, :] = high
        tl[some, :] = low
        for part in range(per_tile):
            outa[i * per_tile + part] = product[part * size : (part + 1) * size]

        @pl.when(c == 0)
        def _():
            for part in range(per_tile):
                block_a(i * per_tile + part).start()

        return 0

    lax.fori_loop(0, tiles, compose, 0)

    @pl.when(c == HUB)
    def _():
        def body(i, _):
            some = pl.ds(pl.multiple_of(i * LANES, LANES), LANES)
            turned = jnp.transpose(outa[:, :, some].reshape(width, LANES))
            for part in range(per_tile):
                outs[i * per_tile + part] = turned[part * size : (part + 1) * size]
                block_s(i * per_tile + part).start()
            return 0

        lax.fori_loop(0, tiles, body, 0)

    split_layer(0)

    loads[3].wait()
    halo_received(slo, shi, "start")

    @pl.when(d < depth - 1)
    def _():
        received(below_in, "below")

    @pl.when(d == depth - 1)
    def _():
        below_in[...] = jnp.zeros(below_in.shape, F32)

    g[0] = rhs[0] - lateral(0, start[0], slo, shi) + vert[1:2, :] * start[1]
    g[1] = rhs[1] - lateral(1, start[1], slo, shi) + below_in[...]
    first = dot3(g[0], dh[0], dl[0])
    o_buf[...] = dot3(g[1] + vert[1:2, :] * first, dh[1], dl[1])

    @pl.when(c == 0)
    def _():
        f_in[...] = jnp.zeros(f_in.shape, F32)
        f_out[...] = o_buf[...]

    step_a = (c // 2) * 4 + c % 2
    last = HUB - c
    step_s = (last // 2) * 4 + last % 2

    def next_f():
        return f_out, f_in, "f_next", "f", d + 1

    def first_down():
        return f_out, eb, "down_hub", "down", d + ROW

    def slot(s, _):
        @pl.when(both(c > 0, s >= step_a, s < step_a + BLOCKS))
        def _():
            b = s - step_a
            some = pl.ds(pl.multiple_of(b * size, size), size)
            block_a(b).wait_recv()
            x = ina[b]
            high, low = split(x)
            ah[some, :] = high
            al[some, :] = low
            product = dot3(x, th[...], tl[...])
            outa[b] = product

            @pl.when(c < HUB)
            def _():
                block_a(b).start()

            @pl.when(c == HUB)
            def _():
                high, low = split(product)
                mh[some, :] = high
                ml[some, :] = low

        @pl.when(s == step_a + 2)
        def _():
            @pl.when(c > 0)
            def _():
                received(f_in, "f")
                f_out[...] = dot3(f_in[...], th[...], tl[...]) + o_buf[...]

            @pl.when(c < HUB)
            def _():
                copy(*next_f()).start()

            @pl.when(both(c == HUB, r == 0))
            def _():
                copy(*first_down()).start()

        @pl.when(both(c < HUB, s >= step_s, s < step_s + BLOCKS))
        def _():
            b = s - step_s
            some = pl.ds(pl.multiple_of(b * size, size), size)
            block_s(b).wait_recv()
            x = ins[b]
            high, low = split(x)
            sh[some, :] = high
            sl[some, :] = low

            @pl.when(c > 0)
            def _():
                outs[b] = dot3(x, th[...], tl[...], True)
                block_s(b).start()

        return 0

    lax.fori_loop(0, (ROW // 2 - 1) * 4 + 1 + BLOCKS, slot, 0)
    waits.append((lambda: c < HUB, next_f))
    waits.append((lambda: both(c == HUB, r == 0), first_down))

    def spread(cond, buf, name):
        @pl.when(c == HUB)
        def _():
            for spoke in (3, 1, 5, 6):
                send(
                    lambda: both(cond(), c == HUB),
                    lambda spoke=spoke: (buf, buf, name + str(spoke), name, base + spoke),
                )

        @pl.when(is_spoke)
        def _():
            send(lambda: both(cond(), is_spoke), lambda: (buf, buf, name + "_pair", name, d - 1))

    @pl.when(r == 0)
    def _():
        e_in[...] = f_in[...]

    @pl.when(r > 0)
    def _():
        received(eb, "down")
        spread(lambda: r > 0, eb, "down")

        @pl.when(both(c == HUB, r < rows - 1))
        def _():
            e_next[...] = dot3(eb[...], mh[...], ml[...]) + f_out[...]
            send(
                lambda: both(c == HUB, r > 0, r < rows - 1),
                lambda: (e_next, eb, "down_hub", "down", d + ROW),
            )

        @pl.when(c == 0)
        def _():
            e_in[...] = eb[...]

        @pl.when(c > 0)
        def _():
            e_in[...] = dot3(eb[...], ah[...], al[...]) + f_in[...]

    entering = vert[0:1, :] * e_in[...]
    y[0] = dot3(g[0] + entering, dh[0], dl[0])
    y[1] = dot3(g[1] + vert[1:2, :] * y[0], dh[1], dl[1])
    halo(y, ylo, yhi, "y")
    halo_received(ylo, yhi, "y")
    h[0] = rhs[0] - lateral(0, y[0], ylo, yhi) + vert[0:1, :] * e_in[...]
    h[1] = rhs[1] - lateral(1, y[1], ylo, yhi) + vert[1:2, :] * y[0]

    above = dot3(h[1], dh[1], dl[1], True)
    p_buf[...] = vert[0:1, :] * dot3(h[0] + vert[1:2, :] * above, dh[0], dl[0], True)

    @pl.when(r > 0)
    def _():
        @pl.when(c == 0)
        def _():
            w_out[...] = p_buf[...]

        @pl.when(c > 0)
        def _():
            w_out[...] = dot3(p_buf[...], ah[...], al[...], True)

        @pl.when(c % 2 == 0)
        def _():
            send(
                lambda: both(r > 0, c % 2 == 0),
                lambda: (w_out, w_pair, "w_pair", "w_pair", d + 1),
            )

        @pl.when(c % 2 == 1)
        def _():
            received(w_pair, "w_pair")
            w_out[...] = w_out[...] + w_pair[...]

        for spoke in (1, 3, 5):

            @pl.when(c == spoke)
            def _():
                send(
                    lambda spoke=spoke: both(r > 0, c == spoke),
                    lambda i=spoke // 2: (w_out, w_hub.at[i], "w_hub", "w" + str(i), base + HUB),
                )

        @pl.when(c == HUB)
        def _():
            for spoke in range(3):
                received(w_hub.at[spoke], "w" + str(spoke))
            o_up[...] = w_out[...] + (w_hub[0] + (w_hub[1] + w_hub[2]))

            @pl.when(r == rows - 1)
            def _():
                send(
                    lambda: both(c == HUB, r > 0, r == rows - 1),
                    lambda: (o_up, ub, "up_hub", "up", d - ROW),
                )

    @pl.when(c == HUB)
    def _():
        g_in[...] = jnp.zeros(g_in.shape, F32)
        g_out[...] = p_buf[...]

    @pl.when(c < HUB)
    def _():
        received(g_in, "g")
        g_out[...] = dot3(g_in[...], th[...], tl[...], True) + p_buf[...]

    @pl.when(c > 0)
    def _():
        send(lambda: c > 0, lambda: (g_out, g_in, "g_prev", "g", d - 1))

    @pl.when(r < rows - 1)
    def _():
        received(ub, "up")
        spread(lambda: r < rows - 1, ub, "up")

        @pl.when(both(c == HUB, r > 0))
        def _():
            u_next[...] = dot3(ub[...], mh[...], ml[...], True) + o_up[...]
            send(
                lambda: both(c == HUB, r > 0, r < rows - 1),
                lambda: (u_next, ub, "up_hub", "up", d - ROW),
            )

        @pl.when(c == HUB)
        def _():
            g_in[...] = ub[...]

        @pl.when(c < HUB)
        def _():
            g_in[...] = g_in[...] + dot3(ub[...], sh[...], sl[...])

    upper = dot3(h[1] + g_in[...], dh[1], dl[1], True)
    out[1] = upper
    out[0] = dot3(h[0] + vert[1:2, :] * upper, dh[0], dl[0], True)

    for cond, args in waits:
        @pl.when(cond())
        def _():
            copy(*args()).wait_send()

    @pl.when(c < HUB)
    def _():
        for b in range(BLOCKS):
            block_a(b).wait_send()

    @pl.when(c > 0)
    def _():
        for b in range(BLOCKS):
            block_s(b).wait_send()


def shards(depth, areas, rhs_field, start_field, inverses, facies, neighbours, lateral_table, vertical_table):
    layers, count, width = rhs_field.shape
    size = width // BLOCKS
    tiles = width // LANES
    field = (layers, count, width)
    matrix = (width, width)
    state = pltpu.VMEM((count, width), F32)

    def blocks():
        return pltpu.VMEM((BLOCKS, size, width), F32)

    def halves():
        return [pltpu.VMEM(matrix, BF16)] * 2

    halo = pltpu.VMEM((layers, count, LANES), F32)
    scratch = (
        [pltpu.VMEM(field, F32)] * 2
        + [pltpu.VMEM((layers,) + matrix, F32)]
        + [pltpu.VMEM((layers,) + matrix, BF16)] * 2
        + halves()
        + [blocks()] + halves() + [blocks()]
        + [blocks()] + halves() + [blocks()]
        + halves()
        + [pltpu.VMEM((layers, tiles, 3 * LANES, LANES), BF16)] * 2
        + [pltpu.VMEM((neighbours.shape[1], layers, width), F32)]
        + [pltpu.VMEM((layers, width), F32)] * 2
        + [halo] * 4
        + [state] * 2
        + [pltpu.VMEM(field, F32)] + [state] * 3
        + [state] * 3
        + [pltpu.VMEM(field, F32)] * 2
        + [state] * 3
        + [pltpu.VMEM((3, count, width), F32)] + [state]
        + [state] * 4
        + [
            pltpu.SemaphoreType.DMA((4,)),
            pltpu.SemaphoreType.DMA((len(SENDS),)),
            pltpu.SemaphoreType.DMA((len(RECVS),)),
        ]
        + [pltpu.SemaphoreType.DMA((BLOCKS,))] * 4
    )
    vmem = pl.BlockSpec(memory_space=pltpu.VMEM)
    smem = pl.BlockSpec(memory_space=pltpu.SMEM)
    hbm = pl.BlockSpec(memory_space=pl.ANY)
    return pl.pallas_call(
        functools.partial(kernel, depth, areas),
        out_shape=jax.ShapeDtypeStruct(field, F32),
        in_specs=[smem, smem, vmem, vmem, hbm, hbm, hbm],
        out_specs=vmem,
        scratch_shapes=scratch,
        compiler_params=pltpu.CompilerParams(
            collective_id=0, has_side_effects=True, vmem_limit_bytes=60 * 1024 * 1024
        ),
        name="sweep",
    )(lateral_table.T, vertical_table, facies, neighbours.T, rhs_field, start_field, inverses)


def solution(mesh):
    return jax.shard_map(
        functools.partial(shards, mesh.shape["depth"], mesh.shape["area"]),
        mesh=mesh,
        in_specs=(
            P("depth", None, "area"),
            P("depth", None, "area"),
            P("depth", "area", None),
            P("depth", "area"),
            P("area", None),
            P(),
            P(),
        ),
        out_specs=P("depth", None, "area"),
        check_vma=False,
    )
```

profile of v0, /device:TPU:38, one launch (start us, length us, event | category | flops | bytes accessed | tf_op | source)
XLA Modules:
  0.0 75.5 jit_solution(9796795960231277004)
XLA Ops:
  0.0 73.9 %sweep.1 = f32[2,32,512]{2,1,0:T(8,128)} custom-call(f32[4,8]{1,0:T(4,128)} %bitcast.3, f32[8]{0:T(128)} %vert_tab.1, s32[2,512]{1,0:T(2,128)} %facies.1, s32[4,512]{1,0:T(4,128)} %bitcast.2, f32[2,32,512]{2,1,0:T(8,128)} %rhs_hbm.1, f32[2,32,512]{2,1,0:T(8,128)} %start_hbm.1, f32[2,512,512]{2,1,0:T(8,128)} %inv_hbm.1), custom_call_target="tpu_custom_call" | custom-call | tf_op jit(solution)/shard_map/sweep/pallas_call | solution.py:544
  73.9 1.6 %copy.9 = f32[2,32,512]{2,1,0:T(8,128)} copy(f32[2,32,512]{2,1,0:T(8,128)} %sweep.1) | data formatting | bytes 262144
where the time goes:
time: 75.7 us; the launch traced here: 75.5 us
  Pallas kernels  73.9 us (98%)
  local copies, waits for them, and re-layouts  1.57 us (2%)
    pallas_call x1, Pallas kernels, shards(): pl.pallas_call(functools.partial(kernel, depth, areas), out_shape=jax.Sha...  73.9 us
    unnamed x1, local copies, waits for them, and re-layouts  1.57 us

commit v1 on v0

--- a/solution.py
+++ b/solution.py
@@ -13,19 +13,21 @@
 HW = 64
 LANES = 128
 ROW = 8
-HUB = ROW - 1
+LAST = ROW - 1
+HUB = 3
+SPOKES = (7, 1, 5)
 BLOCKS = 8
 
 SENDS = (
-    "start_right", "start_left", "below", "f_next", "down_hub", "down6",
-    "down5", "down3", "down1", "down_pair", "y_right", "y_left",
-    "w_pair", "w_hub", "g_prev", "up_hub", "up6", "up5",
-    "up3", "up1", "up_pair",
+    "start_right", "start_left", "below", "f_next", "o_hub", "down_hub",
+    "down7", "down1", "down5", "down2", "down_pair", "y_right",
+    "y_left", "w_pair", "w_hub", "g_prev", "up_hub", "up7",
+    "up1", "up5", "up2", "up_pair",
 )
 RECVS = (
-    "start_lo", "start_hi", "below", "f", "down", "y_lo",
-    "y_hi", "w_pair", "w0", "w1", "w2", "g",
-    "up",
+    "start_lo", "start_hi", "below", "f", "o", "down",
+    "y_lo", "y_hi", "w_pair", "w0", "w1", "w2",
+    "g", "up",
 )
 
 
@@ -35,9 +37,12 @@
 
 
 def dot3(x, w_high, w_low, transposed=False):
-    high, low = split(x)
+    return dot_halves(*split(x), w_high, w_low, transposed)
+
+
+def dot_halves(high, low, w_high, w_low, transposed):
     dims = (((1,), (1 if transposed else 0,)), ((), ()))
-    rows = x.shape[0]
+    rows = high.shape[0]
     both = lax.dot_general(
         jnp.concatenate([high, low], axis=0), w_high, dims, preferred_element_type=F32
     )
@@ -49,9 +54,9 @@
     depth, areas,
     lat_tab, vert_tab, facies, nbrs, rhs_hbm, start_hbm, inv_hbm,
     out,
-    rhs, start, inv, dh, dl, th, tl, ina, ah, al, outa, ins, sh, sl, outs, mh, ml,
-    lat_h, lat_l, wts, wsum, vert, slo, shi, ylo, yhi, below_out, below_in,
-    g, f_in, f_out, o_buf, eb, e_next, e_in, y, h, p_buf, w_out, w_pair, w_hub, o_up,
+    rhs, start, inv, dh, dl, th, tl, ina, ah, al, outa, ins, sh, sl, outs, bh, bl, mh, ml,
+    lat_h, lat_l, wts, wsum, vert, slo, shi, ylo, yhi, to_right, to_left, below_out, below_in,
+    g, f_in, f_out, o_buf, o_down, eb, e_next, e_in, y, h, p_buf, w_out, w_pair, w_hub, o_up,
     g_in, g_out, ub, u_next,
     local, snd, rcv, snd_a, rcv_a, snd_s, rcv_s,
 ):
@@ -108,7 +113,7 @@
         load.start()
 
     barrier = pltpu.get_barrier_semaphore()
-    is_spoke = both(c % 2 == 1, c < HUB)
+    is_spoke = both(c % 2 == 1, c != HUB)
     partners = [
         (d > 0, d - 1, z),
         (d < depth - 1, d + 1, z),
@@ -117,7 +122,7 @@
         (is_spoke, base + HUB, z),
         (both(c == HUB, r > 0), d - ROW, z),
         (both(c == HUB, r < rows - 1), d + ROW, z),
-    ] + [(c == HUB, base + spoke, z) for spoke in (1, 3, 5)]
+    ] + [(c == HUB, base + spoke, z) for spoke in SPOKES]
     for cond, to_depth, to_area in partners:
 
         @pl.when(cond)
@@ -157,13 +162,27 @@
                 lat_h[k, t, first : first + HW, :] = high
                 lat_l[k, t, first : first + HW, :] = low
 
-    def lateral(k, v, low, high):
-        parts = [low[k]] + [v[:, t * LANES : (t + 1) * LANES] for t in range(tiles)] + [high[k]]
-        sums = [
-            dot3(jnp.concatenate(parts[t : t + 3], axis=1), lat_h[k, t], lat_l[k, t])
-            for t in range(tiles)
-        ]
+    def lateral_own(k, v):
+        parts = [v[:, t * LANES : (t + 1) * LANES] for t in range(tiles)]
+        sums = []
+        for t in range(tiles):
+            first, end = max(t - 1, 0), min(t + 2, tiles)
+            rows_of = slice((first - t + 1) * LANES, (end - t + 1) * LANES)
+            x = jnp.concatenate(parts[first:end], axis=1)
+            sums.append(dot3(x, lat_h[k, t, rows_of], lat_l[k, t, rows_of]))
         return wsum[k : k + 1, :] * v - jnp.concatenate(sums, axis=1)
+
+    def add_neighbours(field, low, high):
+        for k in range(2):
+            left, right = low[...], high[...]
+            if k == 1:
+                left, right = pltpu.roll(left, HW, 1), pltpu.roll(right, HW, 1)
+            for t, x, first in ((0, left, 0), (tiles - 1, right, 2 * LANES)):
+                lanes = slice(t * LANES, (t + 1) * LANES)
+                rows_of = slice(first, first + LANES)
+                field[k, :, lanes] = field[k, :, lanes] + dot3(
+                    x, lat_h[k, t, rows_of], lat_l[k, t, rows_of]
+                )
 
     loads[0].wait()
     below_out[...] = vert[0:1, :] * start[0]
@@ -172,19 +191,26 @@
 
     has_left, has_right = z > 0, z < areas - 1
 
-    def halo(field, low, high, name):
+    def halo(field, low, high, name, place):
+        upper_half = lax.broadcasted_iota(jnp.int32, (count, LANES), 1) >= HW
+
         @pl.when(has_right)
         def _():
+            edge = slice(width - LANES, width)
+            to_right[place] = jnp.where(
+                upper_half, field[0, :, edge], pltpu.roll(field[1, :, edge], HW, 1)
+            )
             send(lambda: has_right, lambda: (
-                field.at[:, :, pl.ds(width - LANES, LANES)], low,
-                name + "_right", name + "_lo", d, z + 1,
+                to_right.at[place], low, name + "_right", name + "_lo", d, z + 1,
             ))
 
         @pl.when(has_left)
         def _():
+            to_left[place] = jnp.where(
+                upper_half, pltpu.roll(field[1, :, :LANES], HW, 1), field[0, :, :LANES]
+            )
             send(lambda: has_left, lambda: (
-                field.at[:, :, pl.ds(0, LANES)], high,
-                name + "_left", name + "_hi", d, z - 1,
+                to_left.at[place], high, name + "_left", name + "_hi", d, z - 1,
             ))
 
         @pl.when(jnp.logical_not(has_left))
@@ -204,7 +230,7 @@
         def _():
             received(high, name + "_hi")
 
-    halo(start, slo, shi, "start")
+    halo(start, slo, shi, "start", 0)
 
     @pl.when(d > 0)
     def _():
@@ -245,7 +271,7 @@
 
     lax.fori_loop(0, tiles, compose, 0)
 
-    @pl.when(c == HUB)
+    @pl.when(c == LAST)
     def _():
         def body(i, _):
             some = pl.ds(pl.multiple_of(i * LANES, LANES), LANES)
@@ -259,36 +285,36 @@
 
     split_layer(0)
 
-    loads[3].wait()
-    halo_received(slo, shi, "start")
-
-    @pl.when(d < depth - 1)
-    def _():
-        received(below_in, "below")
-
-    @pl.when(d == depth - 1)
-    def _():
-        below_in[...] = jnp.zeros(below_in.shape, F32)
-
-    g[0] = rhs[0] - lateral(0, start[0], slo, shi) + vert[1:2, :] * start[1]
-    g[1] = rhs[1] - lateral(1, start[1], slo, shi) + below_in[...]
-    first = dot3(g[0], dh[0], dl[0])
-    o_buf[...] = dot3(g[1] + vert[1:2, :] * first, dh[1], dl[1])
-
-    @pl.when(c == 0)
-    def _():
-        f_in[...] = jnp.zeros(f_in.shape, F32)
-        f_out[...] = o_buf[...]
+    def own_part():
+        loads[3].wait()
+        g[0] = rhs[0] - lateral_own(0, start[0]) + vert[1:2, :] * start[1]
+        g[1] = rhs[1] - lateral_own(1, start[1])
+        halo_received(slo, shi, "start")
+        add_neighbours(g, slo, shi)
+
+        @pl.when(d < depth - 1)
+        def _():
+            received(below_in, "below")
+            g[1] = g[1] + below_in[...]
+
+        first = dot3(g[0], dh[0], dl[0])
+        o_buf[...] = dot3(g[1] + vert[1:2, :] * first, dh[1], dl[1])
+
+        @pl.when(c == 0)
+        def _():
+            f_in[...] = jnp.zeros(f_in.shape, F32)
+            f_out[...] = o_buf[...]
 
     step_a = (c // 2) * 4 + c % 2
-    last = HUB - c
+    last = LAST - c
     step_s = (last // 2) * 4 + last % 2
+    middle = (HUB // 2) * 4 + 4 + BLOCKS - 1
 
     def next_f():
         return f_out, f_in, "f_next", "f", d + 1
 
-    def first_down():
-        return f_out, eb, "down_hub", "down", d + ROW
+    def row_offset():
+        return f_out, o_down, "o_hub", "o", base + HUB
 
     def slot(s, _):
         @pl.when(both(c > 0, s >= step_a, s < step_a + BLOCKS))
@@ -296,63 +322,73 @@
             b = s - step_a
             some = pl.ds(pl.multiple_of(b * size, size), size)
             block_a(b).wait_recv()
-            x = ina[b]
-            high, low = split(x)
+            high, low = split(ina[b])
             ah[some, :] = high
             al[some, :] = low
-            product = dot3(x, th[...], tl[...])
-            outa[b] = product
-
-            @pl.when(c < HUB)
+
+            @pl.when(c < LAST)
             def _():
+                product = dot_halves(high, low, th[...], tl[...], False)
+                outa[b] = product
                 block_a(b).start()
 
-            @pl.when(c == HUB)
-            def _():
-                high, low = split(product)
-                mh[some, :] = high
-                ml[some, :] = low
-
-        @pl.when(s == step_a + 2)
+                @pl.when(c == HUB)
+                def _():
+                    high, low = split(product)
+                    bh[some, :] = high
+                    bl[some, :] = low
+
+        @pl.when(s == 1)
+        def _():
+            own_part()
+
+        @pl.when(s == step_a + 1)
         def _():
             @pl.when(c > 0)
             def _():
                 received(f_in, "f")
                 f_out[...] = dot3(f_in[...], th[...], tl[...]) + o_buf[...]
 
-            @pl.when(c < HUB)
+            @pl.when(c < LAST)
             def _():
                 copy(*next_f()).start()
 
-            @pl.when(both(c == HUB, r == 0))
+            @pl.when(both(c == LAST, r < rows - 1))
             def _():
-                copy(*first_down()).start()
-
-        @pl.when(both(c < HUB, s >= step_s, s < step_s + BLOCKS))
+                copy(*row_offset()).start()
+
+        @pl.when(both(c < LAST, s >= step_s, s < step_s + BLOCKS))
         def _():
             b = s - step_s
             some = pl.ds(pl.multiple_of(b * size, size), size)
             block_s(b).wait_recv()
-            x = ins[b]
-            high, low = split(x)
+            high, low = split(ins[b])
             sh[some, :] = high
             sl[some, :] = low
 
             @pl.when(c > 0)
             def _():
-                outs[b] = dot3(x, th[...], tl[...], True)
+                outs[b] = dot_halves(high, low, th[...], tl[...], True)
                 block_s(b).start()
 
+        @pl.when(both(c == HUB, s > middle - tiles, s <= middle))
+        def _():
+            i = s - (middle - tiles + 1)
+            some = pl.ds(pl.multiple_of(i * LANES, LANES), LANES)
+            high, low = split(dot_halves(sh[some, :], sl[some, :], bh[...], bl[...], True))
+            mh[some, :] = high
+            ml[some, :] = low
+
         return 0
 
     lax.fori_loop(0, (ROW // 2 - 1) * 4 + 1 + BLOCKS, slot, 0)
-    waits.append((lambda: c < HUB, next_f))
-    waits.append((lambda: both(c == HUB, r == 0), first_down))
+    waits.append((lambda: c < LAST, next_f))
+    waits.append((lambda: both(c == LAST, r < rows - 1), row_offset))
 
     def spread(cond, buf, name):
         @pl.when(c == HUB)
         def _():
-            for spoke in (3, 1, 5, 6):
+            for spoke in SPOKES + (HUB - 1,):
                 send(
                     lambda: both(cond(), c == HUB),
                     lambda spoke=spoke: (buf, buf, name + str(spoke), name, base + spoke),
@@ -362,6 +398,17 @@
         def _():
             send(lambda: both(cond(), is_spoke), lambda: (buf, buf, name + "_pair", name, d - 1))
 
+    @pl.when(both(c == HUB, r < rows - 1))
+    def _():
+        received(o_down, "o")
+
+        @pl.when(r == 0)
+        def _():
+            send(
+                lambda: both(c == HUB, r == 0, r < rows - 1),
+                lambda: (o_down, eb, "down_hub", "down", d + ROW),
+            )
+
     @pl.when(r == 0)
     def _():
         e_in[...] = f_in[...]
@@ -373,7 +420,7 @@
 
         @pl.when(both(c == HUB, r < rows - 1))
         def _():
-            e_next[...] = dot3(eb[...], mh[...], ml[...]) + f_out[...]
+            e_next[...] = dot3(eb[...], mh[...], ml[...], True) + o_down[...]
             send(
                 lambda: both(c == HUB, r > 0, r < rows - 1),
                 lambda: (e_next, eb, "down_hub", "down", d + ROW),
@@ -390,13 +437,23 @@
     entering = vert[0:1, :] * e_in[...]
     y[0] = dot3(g[0] + entering, dh[0], dl[0])
     y[1] = dot3(g[1] + vert[1:2, :] * y[0], dh[1], dl[1])
-    halo(y, ylo, yhi, "y")
+    halo(y, ylo, yhi, "y", 1)
+    h[0] = rhs[0] - lateral_own(0, y[0]) + entering
+    h[1] = rhs[1] - lateral_own(1, y[1]) + vert[1:2, :] * y[0]
     halo_received(ylo, yhi, "y")
-    h[0] = rhs[0] - lateral(0, y[0], ylo, yhi) + vert[0:1, :] * e_in[...]
-    h[1] = rhs[1] - lateral(1, y[1], ylo, yhi) + vert[1:2, :] * y[0]
+    add_neighbours(h, ylo, yhi)
+
+    def next_g():
+        return g_out, g_in, "g_prev", "g", d - 1
 
     above = dot3(h[1], dh[1], dl[1], True)
     p_buf[...] = vert[0:1, :] * dot3(h[0] + vert[1:2, :] * above, dh[0], dl[0], True)
+
+    @pl.when(c == LAST)
+    def _():
+        g_in[...] = jnp.zeros(g_in.shape, F32)
+        g_out[...] = p_buf[...]
+        copy(*next_g()).start()
 
     @pl.when(r > 0)
     def _():
@@ -420,13 +477,13 @@
             received(w_pair, "w_pair")
             w_out[...] = w_out[...] + w_pair[...]
 
-        for spoke in (1, 3, 5):
+        for i, spoke in enumerate(SPOKES):
 
             @pl.when(c == spoke)
             def _():
                 send(
                     lambda spoke=spoke: both(r > 0, c == spoke),
-                    lambda i=spoke // 2: (w_out, w_hub.at[i], "w_hub", "w" + str(i), base + HUB),
+                    lambda i=i: (w_out, w_hub.at[i], "w_hub", "w" + str(i), base + HUB),
                 )
 
         @pl.when(c == HUB)
@@ -442,19 +499,16 @@
                     lambda: (o_up, ub, "up_hub", "up", d - ROW),
                 )
 
-    @pl.when(c == HUB)
-    def _():
-        g_in[...] = jnp.zeros(g_in.shape, F32)
-        g_out[...] = p_buf[...]
-
-    @pl.when(c < HUB)
+    @pl.when(c < LAST)
     def _():
         received(g_in, "g")
-        g_out[...] = dot3(g_in[...], th[...], tl[...], True) + p_buf[...]
-
-    @pl.when(c > 0)
-    def _():
-        send(lambda: c > 0, lambda: (g_out, g_in, "g_prev", "g", d - 1))
+
+        @pl.when(c > 0)
+        def _():
+            g_out[...] = dot3(g_in[...], th[...], tl[...], True) + p_buf[...]
+            copy(*next_g()).start()
+
+    waits.append((lambda: c > 0, next_g))
 
     @pl.when(r < rows - 1)
     def _():
@@ -463,17 +517,17 @@
 
         @pl.when(both(c == HUB, r > 0))
         def _():
-            u_next[...] = dot3(ub[...], mh[...], ml[...], True) + o_up[...]
+            u_next[...] = dot3(ub[...], mh[...], ml[...]) + o_up[...]
             send(
                 lambda: both(c == HUB, r > 0, r < rows - 1),
                 lambda: (u_next, ub, "up_hub", "up", d - ROW),
             )
 
-        @pl.when(c == HUB)
+        @pl.when(c == LAST)
         def _():
             g_in[...] = ub[...]
 
-        @pl.when(c < HUB)
+        @pl.when(c < LAST)
         def _():
             g_in[...] = g_in[...] + dot3(ub[...], sh[...], sl[...])
 
@@ -486,7 +540,7 @@
         def _():
             copy(*args()).wait_send()
 
-    @pl.when(c < HUB)
+    @pl.when(c < LAST)
     def _():
         for b in range(BLOCKS):
             block_a(b).wait_send()
@@ -511,7 +565,7 @@
     def halves():
         return [pltpu.VMEM(matrix, BF16)] * 2
 
-    halo = pltpu.VMEM((layers, count, LANES), F32)
+    halo = pltpu.VMEM((count, LANES), F32)
     scratch = (
         [pltpu.VMEM(field, F32)] * 2
         + [pltpu.VMEM((layers,) + matrix, F32)]
@@ -519,13 +573,14 @@
         + halves()
         + [blocks()] + halves() + [blocks()]
         + [blocks()] + halves() + [blocks()]
-        + halves()
+        + halves() * 2
         + [pltpu.VMEM((layers, tiles, 3 * LANES, LANES), BF16)] * 2
         + [pltpu.VMEM((neighbours.shape[1], layers, width), F32)]
         + [pltpu.VMEM((layers, width), F32)] * 2
         + [halo] * 4
+        + [pltpu.VMEM((2, count, LANES), F32)] * 2
         + [state] * 2
-        + [pltpu.VMEM(field, F32)] + [state] * 3
+        + [pltpu.VMEM(field, F32)] + [state] * 4
         + [state] * 3
         + [pltpu.VMEM(field, F32)] * 2
         + [state] * 3

time: 75.7 us -> 70.2 us (0.927)
  the two profiles are of different devices: /device:TPU:38 before, /device:TPU:96 now
where the time goes in v1:
time: 70.2 us; the launch traced here: 70 us
  Pallas kernels  68.4 us (97%)
  local copies, waits for them, and re-layouts  1.57 us (2%)
    pallas_call x1, Pallas kernels, shards(): pl.pallas_call(functools.partial(kernel, depth, areas), out_shape=jax.Sha...  68.4 us
    unnamed x1, local copies, waits for them, and re-layouts  1.57 us

profile of v1, /device:TPU:96, one launch (start us, length us, event | category | flops | bytes accessed | tf_op | source)
XLA Modules:
  0.0 70.0 jit_solution(13739539601727672616)
XLA Ops:
  0.0 68.4 %sweep.1 = f32[2,32,512]{2,1,0:T(8,128)} custom-call(f32[4,8]{1,0:T(4,128)} %bitcast.3, f32[8]{0:T(128)} %vert_tab.1, s32[2,512]{1,0:T(2,128)} %facies.1, s32[4,512]{1,0:T(4,128)} %bitcast.2, f32[2,32,512]{2,1,0:T(8,128)} %rhs_hbm.1, f32[2,32,512]{2,1,0:T(8,128)} %start_hbm.1, f32[2,512,512]{2,1,0:T(8,128)} %inv_hbm.1), custom_call_target="tpu_custom_call" | custom-call | tf_op jit(solution)/shard_map/sweep/pallas_call | solution.py:599
  68.4 1.6 %copy.9 = f32[2,32,512]{2,1,0:T(8,128)} copy(f32[2,32,512]{2,1,0:T(8,128)} %sweep.1) | data formatting | bytes 262144

commit v2 on v1

--- a/solution.py
+++ b/solution.py
@@ -20,8 +20,8 @@
 
 SENDS = (
     "start_right", "start_left", "below", "f_next", "o_hub", "down_hub",
-    "down7", "down1", "down5", "down2", "down_pair", "y_right",
-    "y_left", "w_pair", "w_hub", "g_prev", "up_hub", "up7",
+    "down_far", "down1", "down5", "down2", "down_pair", "y_right",
+    "y_left", "w_pair", "w_hub", "g_prev", "up_hub", "up_far",
     "up1", "up5", "up2", "up_pair",
 )
 RECVS = (
@@ -54,7 +54,7 @@
     depth, areas,
     lat_tab, vert_tab, facies, nbrs, rhs_hbm, start_hbm, inv_hbm,
     out,
-    rhs, start, inv, dh, dl, th, tl, ina, ah, al, outa, ins, sh, sl, outs, bh, bl, mh, ml,
+    rhs, start, inv, dh, dl, dth, dtl, th, tl, tth, ttl, ina, ah, al, outa, ins, sh, sl, outs, bh, bl, mh, ml,
     lat_h, lat_l, wts, wsum, vert, slo, shi, ylo, yhi, to_right, to_left, below_out, below_in,
     g, f_in, f_out, o_buf, o_down, eb, e_next, e_in, y, h, p_buf, w_out, w_pair, w_hub, o_up,
     g_in, g_out, ub, u_next,
@@ -122,6 +122,12 @@
         (is_spoke, base + HUB, z),
         (both(c == HUB, r > 0), d - ROW, z),
         (both(c == HUB, r < rows - 1), d + ROW, z),
+        (both(c == HUB, r > 0), d - ROW + (LAST - HUB), z),
+        (both(c == HUB, r < rows - 1), d + ROW + (LAST - HUB), z),
+        (both(c == LAST, r > 0), d - ROW - (LAST - HUB), z),
+        (both(c == LAST, r < rows - 1), d + ROW - (LAST - HUB), z),
+        (both(c == LAST, r == 0, r < rows - 1), d + ROW, z),
+        (both(c == LAST, r == 1), d - ROW, z),
     ] + [(c == HUB, base + spoke, z) for spoke in SPOKES]
     for cond, to_depth, to_area in partners:
 
@@ -261,6 +267,11 @@
         tl[some, :] = low
         for part in range(per_tile):
             outa[i * per_tile + part] = product[part * size : (part + 1) * size]
+        turned = jnp.transpose(product)
+        outs[:, :, some] = turned.reshape(BLOCKS, size, LANES)
+        high, low = split(turned)
+        tth[:, some] = high
+        ttl[:, some] = low
 
         @pl.when(c == 0)
         def _():
@@ -273,15 +284,8 @@
 
     @pl.when(c == LAST)
     def _():
-        def body(i, _):
-            some = pl.ds(pl.multiple_of(i * LANES, LANES), LANES)
-            turned = jnp.transpose(outa[:, :, some].reshape(width, LANES))
-            for part in range(per_tile):
-                outs[i * per_tile + part] = turned[part * size : (part + 1) * size]
-                block_s(i * per_tile + part).start()
-            return 0
-
-        lax.fori_loop(0, tiles, body, 0)
+        for b in range(BLOCKS):
+            block_s(b).start()
 
     split_layer(0)
 
@@ -316,6 +320,14 @@
     def row_offset():
         return f_out, o_down, "o_hub", "o", base + HUB
 
+    def first_offset():
+        return f_out, eb, "down_hub", "down", base + ROW + HUB
+
+    def first_far():
+        return f_out, eb, "down_far", "down", base + ROW + LAST
+
+    step_f = jnp.maximum(step_a + 1, 2)
+
     def slot(s, _):
         @pl.when(both(c > 0, s >= step_a, s < step_a + BLOCKS))
         def _():
@@ -338,25 +350,6 @@
                     bh[some, :] = high
                     bl[some, :] = low
 
-        @pl.when(s == 1)
-        def _():
-            own_part()
-
-        @pl.when(s == step_a + 1)
-        def _():
-            @pl.when(c > 0)
-            def _():
-                received(f_in, "f")
-                f_out[...] = dot3(f_in[...], th[...], tl[...]) + o_buf[...]
-
-            @pl.when(c < LAST)
-            def _():
-                copy(*next_f()).start()
-
-            @pl.when(both(c == LAST, r < rows - 1))
-            def _():
-                copy(*row_offset()).start()
-
         @pl.when(both(c < LAST, s >= step_s, s < step_s + BLOCKS))
         def _():
             b = s - step_s
@@ -368,8 +361,40 @@
 
             @pl.when(c > 0)
             def _():
-                outs[b] = dot_halves(high, low, th[...], tl[...], True)
+                outs[b] = dot_halves(high, low, tth[...], ttl[...], False)
                 block_s(b).start()
+
+        @pl.when(s == 2)
+        def _():
+            own_part()
+
+        @pl.when(s == step_f)
+        def _():
+            @pl.when(c > 0)
+            def _():
+                received(f_in, "f")
+                f_out[...] = dot3(f_in[...], th[...], tl[...]) + o_buf[...]
+
+            @pl.when(c < LAST)
+            def _():
+                copy(*next_f()).start()
+
+            @pl.when(both(c == LAST, r > 0, r < rows - 1))
+            def _():
+                copy(*row_offset()).start()
+
+            @pl.when(both(c == LAST, r == 0, r < rows - 1))
+            def _():
+                copy(*first_offset()).start()
+                copy(*first_far()).start()
+
+        @pl.when(both(s > 2, s < 5))
+        def _():
+            k = s - 3
+            for t in range(tiles):
+                lanes = slice(t * LANES, (t + 1) * LANES)
+                dth[k, :, lanes] = jnp.transpose(dh[k, lanes, :])
+                dtl[k, :, lanes] = jnp.transpose(dl[k, lanes, :])
 
         @pl.when(both(c == HUB, s > middle - tiles, s <= middle))
         def _():
@@ -383,12 +408,14 @@
 
     lax.fori_loop(0, (ROW // 2 - 1) * 4 + 1 + BLOCKS, slot, 0)
     waits.append((lambda: c < LAST, next_f))
-    waits.append((lambda: both(c == LAST, r < rows - 1), row_offset))
+    waits.append((lambda: both(c == LAST, r > 0, r < rows - 1), row_offset))
+    waits.append((lambda: both(c == LAST, r == 0, r < rows - 1), first_offset))
+    waits.append((lambda: both(c == LAST, r == 0, r < rows - 1), first_far))
 
     def spread(cond, buf, name):
         @pl.when(c == HUB)
         def _():
-            for spoke in SPOKES + (HUB - 1,):
+            for spoke in (1, 5, HUB - 1):
                 send(
                     lambda: both(cond(), c == HUB),
                     lambda spoke=spoke: (buf, buf, name + str(spoke), name, base + spoke),
@@ -398,17 +425,6 @@
         def _():
             send(lambda: both(cond(), is_spoke), lambda: (buf, buf, name + "_pair", name, d - 1))
 
-    @pl.when(both(c == HUB, r < rows - 1))
-    def _():
-        received(o_down, "o")
-
-        @pl.when(r == 0)
-        def _():
-            send(
-                lambda: both(c == HUB, r == 0, r < rows - 1),
-                lambda: (o_down, eb, "down_hub", "down", d + ROW),
-            )
-
     @pl.when(r == 0)
     def _():
         e_in[...] = f_in[...]
@@ -420,11 +436,13 @@
 
         @pl.when(both(c == HUB, r < rows - 1))
         def _():
+            received(o_down, "o")
             e_next[...] = dot3(eb[...], mh[...], ml[...], True) + o_down[...]
-            send(
-                lambda: both(c == HUB, r > 0, r < rows - 1),
-                lambda: (e_next, eb, "down_hub", "down", d + ROW),
-            )
+            for name, to in (("down_hub", HUB), ("down_far", LAST)):
+                send(
+                    lambda: both(c == HUB, r > 0, r < rows - 1),
+                    lambda name=name, to=to: (e_next, eb, name, "down", base + ROW + to),
+                )
 
         @pl.when(c == 0)
         def _():
@@ -446,8 +464,8 @@
     def next_g():
         return g_out, g_in, "g_prev", "g", d - 1
 
-    above = dot3(h[1], dh[1], dl[1], True)
-    p_buf[...] = vert[0:1, :] * dot3(h[0] + vert[1:2, :] * above, dh[0], dl[0], True)
+    above = dot3(h[1], dth[1], dtl[1])
+    p_buf[...] = vert[0:1, :] * dot3(h[0] + vert[1:2, :] * above, dth[0], dtl[0])
 
     @pl.when(c == LAST)
     def _():
@@ -494,10 +512,11 @@
 
             @pl.when(r == rows - 1)
             def _():
-                send(
-                    lambda: both(c == HUB, r > 0, r == rows - 1),
-                    lambda: (o_up, ub, "up_hub", "up", d - ROW),
-                )
+                for name, to in (("up_hub", HUB), ("up_far", LAST)):
+                    send(
+                        lambda: both(c == HUB, r > 0, r == rows - 1),
+                        lambda name=name, to=to: (o_up, ub, name, "up", base - ROW + to),
+                    )
 
     @pl.when(c < LAST)
     def _():
@@ -505,7 +524,7 @@
 
         @pl.when(c > 0)
         def _():
-            g_out[...] = dot3(g_in[...], th[...], tl[...], True) + p_buf[...]
+            g_out[...] = dot3(g_in[...], tth[...], ttl[...]) + p_buf[...]
             copy(*next_g()).start()
 
     waits.append((lambda: c > 0, next_g))
@@ -518,10 +537,11 @@
         @pl.when(both(c == HUB, r > 0))
         def _():
             u_next[...] = dot3(ub[...], mh[...], ml[...]) + o_up[...]
-            send(
-                lambda: both(c == HUB, r > 0, r < rows - 1),
-                lambda: (u_next, ub, "up_hub", "up", d - ROW),
-            )
+            for name, to in (("up_hub", HUB), ("up_far", LAST)):
+                send(
+                    lambda: both(c == HUB, r > 0, r < rows - 1),
+                    lambda name=name, to=to: (u_next, ub, name, "up", base - ROW + to),
+                )
 
         @pl.when(c == LAST)
         def _():
@@ -531,9 +551,9 @@
         def _():
             g_in[...] = g_in[...] + dot3(ub[...], sh[...], sl[...])
 
-    upper = dot3(h[1] + g_in[...], dh[1], dl[1], True)
+    upper = dot3(h[1] + g_in[...], dth[1], dtl[1])
     out[1] = upper
-    out[0] = dot3(h[0] + vert[1:2, :] * upper, dh[0], dl[0], True)
+    out[0] = dot3(h[0] + vert[1:2, :] * upper, dth[0], dtl[0])
 
     for cond, args in waits:
         @pl.when(cond())
@@ -569,8 +589,8 @@
     scratch = (
         [pltpu.VMEM(field, F32)] * 2
         + [pltpu.VMEM((layers,) + matrix, F32)]
-        + [pltpu.VMEM((layers,) + matrix, BF16)] * 2
-        + halves()
+        + [pltpu.VMEM((layers,) + matrix, BF16)] * 4
+        + halves() * 2
         + [blocks()] + halves() + [blocks()]
         + [blocks()] + halves() + [blocks()]
         + halves() * 2
@@ -598,7 +618,7 @@
     hbm = pl.BlockSpec(memory_space=pl.ANY)
     return pl.pallas_call(
         functools.partial(kernel, depth, areas),
-        out_shape=jax.ShapeDtypeStruct(field, F32),
+        out_shape=pltpu.VMEM(field, F32),
         in_specs=[smem, smem, vmem, vmem, hbm, hbm, hbm],
         out_specs=vmem,
         scratch_shapes=scratch,

time: 70.2 us -> 63 us (0.90)
  the two profiles are of different devices: /device:TPU:96 before, /device:TPU:224 now
where the time goes in v2:
time: 63 us; the launch traced here: 62.8 us
  Pallas kernels  62.2 us (99%)
  local copies, waits for them, and re-layouts  0.66 us (1%)
    pallas_call x1, Pallas kernels, shards(): pl.pallas_call(functools.partial(kernel, depth, areas), out_shape=pltpu.V...  62.2 us

profile of v2, /device:TPU:224, one launch (start us, length us, event | category | flops | bytes accessed | tf_op | source)
XLA Modules:
  0.0 62.8 jit_solution(9810238831041924243)
XLA Ops:
  0.0 62.2 %sweep.1 = f32[2,32,512]{2,1,0:T(8,128)S(1)} custom-call(f32[4,8]{1,0:T(4,128)} %bitcast.3, f32[8]{0:T(128)} %vert_tab.1, s32[2,512]{1,0:T(2,128)} %facies.1, s32[4,512]{1,0:T(4,128)} %bitcast.2, f32[2,32,512]{2,1,0:T(8,128)} %rhs_hbm.1, f32[2,32,512]{2,1,0:T(8,128)} %start_hbm.1, f32[2,512,512]{2,1,0:T(8,128)} %inv_hbm.1), custom_call_target="tpu_custom_call" | custom-call | tf_op jit(solution)/shard_map/sweep/pallas_call | solution.py:619
  62.2 0.7 %copy.9 = f32[2,32,512]{2,1,0:T(8,128)} copy(f32[2,32,512]{2,1,0:T(8,128)S(1)} %sweep.1) | data formatting | bytes 262144

commit v3 on v2

--- a/solution.py
+++ b/solution.py
@@ -16,6 +16,7 @@
 LAST = ROW - 1
 HUB = 3
 SPOKES = (7, 1, 5)
+OUTER = (6, 0, 4)
 BLOCKS = 8
 
 SENDS = (
@@ -27,7 +28,7 @@
 RECVS = (
     "start_lo", "start_hi", "below", "f", "o", "down",
     "y_lo", "y_hi", "w_pair", "w0", "w1", "w2",
-    "g", "up",
+    "w3", "w4", "w5", "g", "up",
 )
 
 
@@ -69,17 +70,24 @@
     tiles = width // LANES
     size = width // BLOCKS
     base = r * ROW
+    has_a = r > 0
+    has_s = r < rows - 1
     waits = []
 
     def both(*conds):
         return functools.reduce(jnp.logical_and, conds)
 
-    def copy(src, dst, send, recv, depth_id, area_id=None):
+    def half(part):
+        return pl.ds(part * (count // 2), count // 2)
+
+    def copy(src, dst, send, recv, depth_id, area_id=None, part=None):
+        if part is not None:
+            src, dst = src.at[half(part)], dst.at[half(part)]
         return pltpu.make_async_remote_copy(
             src_ref=src,
             dst_ref=dst,
-            send_sem=snd.at[SENDS.index(send)],
-            recv_sem=rcv.at[RECVS.index(recv)],
+            send_sem=snd.at[SENDS.index(send), part or 0],
+            recv_sem=rcv.at[RECVS.index(recv), part or 0],
             device_id=(depth_id, z if area_id is None else area_id),
             device_id_type=MESH,
         )
@@ -88,8 +96,8 @@
         waits.append((cond, args))
         copy(*args()).start()
 
-    def received(dst, recv):
-        copy(dst, dst, SENDS[0], recv, d).wait_recv()
+    def received(dst, recv, part=None):
+        copy(dst, dst, SENDS[0], recv, d, None, part).wait_recv()
 
     def block_a(b):
         return pltpu.make_async_remote_copy(
@@ -128,7 +136,8 @@
         (both(c == LAST, r < rows - 1), d + ROW - (LAST - HUB), z),
         (both(c == LAST, r == 0, r < rows - 1), d + ROW, z),
         (both(c == LAST, r == 1), d - ROW, z),
-    ] + [(c == HUB, base + spoke, z) for spoke in SPOKES]
+        (both(c % 2 == 0, c != HUB - 1), base + HUB, z),
+    ] + [(c == HUB, base + other, z) for other in SPOKES + OUTER]
     for cond, to_depth, to_area in partners:
 
         @pl.when(cond)
@@ -253,39 +262,68 @@
         lax.fori_loop(0, tiles, body, 0)
 
     per_tile = LANES // size
-    loads[1].wait()
-    split_layer(1)
-    loads[2].wait()
+
+    def scaled_rows(some):
+        scale = jnp.transpose(jnp.broadcast_to(vert[0:1, some], (LANES, LANES)))
+        return inv[0, some, :] * vert[1:2, :] * jnp.concatenate([scale] * tiles, axis=1)
 
     def compose(i, _):
         some = pl.ds(pl.multiple_of(i * LANES, LANES), LANES)
-        scale = jnp.transpose(jnp.broadcast_to(vert[0:1, some], (LANES, LANES)))
-        left = inv[0, some, :] * vert[1:2, :] * jnp.concatenate([scale] * tiles, axis=1)
-        product = dot3(left, dh[1], dl[1])
+        product = dot3(scaled_rows(some), dh[1], dl[1])
         high, low = split(product)
         th[some, :] = high
         tl[some, :] = low
         for part in range(per_tile):
             outa[i * per_tile + part] = product[part * size : (part + 1) * size]
-        turned = jnp.transpose(product)
-        outs[:, :, some] = turned.reshape(BLOCKS, size, LANES)
-        high, low = split(turned)
-        tth[:, some] = high
-        ttl[:, some] = low
-
-        @pl.when(c == 0)
+
+        @pl.when(both(c == 0, has_a))
         def _():
             for part in range(per_tile):
                 block_a(i * per_tile + part).start()
 
         return 0
 
-    lax.fori_loop(0, tiles, compose, 0)
-
-    @pl.when(c == LAST)
-    def _():
-        for b in range(BLOCKS):
-            block_s(b).start()
+    def turn(i, _):
+        some = pl.ds(pl.multiple_of(i * LANES, LANES), LANES)
+        tth[:, some] = jnp.transpose(th[some, :])
+        ttl[:, some] = jnp.transpose(tl[some, :])
+        return 0
+
+    def halves_of_left(i, _):
+        some = pl.ds(pl.multiple_of(i * LANES, LANES), LANES)
+        high, low = split(scaled_rows(some))
+        sh[some, :] = high
+        sl[some, :] = low
+        return 0
+
+    def compose_turned(i, _):
+        some = pl.ds(pl.multiple_of(i * LANES, LANES), LANES)
+        product = dot3(jnp.transpose(inv[1, :, some]), sh[...], sl[...], True)
+        for part in range(per_tile):
+            outs[i * per_tile + part] = product[part * size : (part + 1) * size]
+            block_s(i * per_tile + part).start()
+        high, low = split(product)
+        tth[some, :] = high
+        ttl[some, :] = low
+        th[:, some] = jnp.transpose(high)
+        tl[:, some] = jnp.transpose(low)
+        return 0
+
+    starts_s = both(c == LAST, has_s)
+    loads[1].wait()
+    loads[2].wait()
+
+    @pl.when(starts_s)
+    def _():
+        lax.fori_loop(0, tiles, halves_of_left, 0)
+        lax.fori_loop(0, tiles, compose_turned, 0)
+        split_layer(1)
+
+    @pl.when(jnp.logical_not(starts_s))
+    def _():
+        split_layer(1)
+        lax.fori_loop(0, tiles, compose, 0)
+        lax.fori_loop(0, tiles, turn, 0)
 
     split_layer(0)
 
@@ -314,22 +352,23 @@
     step_s = (last // 2) * 4 + last % 2
     middle = (HUB // 2) * 4 + 4 + BLOCKS - 1
 
-    def next_f():
-        return f_out, f_in, "f_next", "f", d + 1
-
-    def row_offset():
-        return f_out, o_down, "o_hub", "o", base + HUB
-
-    def first_offset():
-        return f_out, eb, "down_hub", "down", base + ROW + HUB
-
-    def first_far():
-        return f_out, eb, "down_far", "down", base + ROW + LAST
-
-    step_f = jnp.maximum(step_a + 1, 2)
+    def next_f(part):
+        return f_out, f_in, "f_next", "f", d + 1, None, part
+
+    def row_offset(part):
+        return f_out, o_down, "o_hub", "o", base + HUB, None, part
+
+    def first_offset(part):
+        return f_out, eb, "down_hub", "down", base + ROW + HUB, None, part
+
+    def first_far(part):
+        return f_out, eb, "down_far", "down", base + ROW + LAST, None, part
+
+    step_f = jnp.where(has_a, jnp.maximum(step_a + 1, 2), jnp.maximum(step_a, 1))
+    step_own = jnp.where(has_a, jnp.where(c <= 1, 2, 3), 1)
 
     def slot(s, _):
-        @pl.when(both(c > 0, s >= step_a, s < step_a + BLOCKS))
+        @pl.when(both(c > 0, has_a, s >= step_a, s < step_a + BLOCKS))
         def _():
             b = s - step_a
             some = pl.ds(pl.multiple_of(b * size, size), size)
@@ -350,7 +389,38 @@
                     bh[some, :] = high
                     bl[some, :] = low
 
-        @pl.when(both(c < LAST, s >= step_s, s < step_s + BLOCKS))
+        @pl.when(s == step_own)
+        def _():
+            own_part()
+
+        @pl.when(s == step_f)
+        def _():
+            for part in range(2):
+                some = half(part)
+
+                @pl.when(c > 0)
+                def _():
+                    received(f_in, "f", part)
+                    f_out[some] = dot3(f_in[some], th[...], tl[...]) + o_buf[some]
+
+                @pl.when(c < LAST)
+                def _():
+                    copy(*next_f(part)).start()
+
+                @pl.when(both(c == LAST, r > 0, r < rows - 1))
+                def _():
+                    copy(*row_offset(part)).start()
+
+                @pl.when(both(c == LAST, r == 0, r < rows - 1))
+                def _():
+                    copy(*first_offset(part)).start()
+
+            @pl.when(both(c == LAST, r == 0, r < rows - 1))
+            def _():
+                for part in range(2):
+                    copy(*first_far(part)).start()
+
+        @pl.when(both(c < LAST, has_s, s >= step_s, s < step_s + BLOCKS))
         def _():
             b = s - step_s
             some = pl.ds(pl.multiple_of(b * size, size), size)
@@ -364,39 +434,15 @@
                 outs[b] = dot_halves(high, low, tth[...], ttl[...], False)
                 block_s(b).start()
 
-        @pl.when(s == 2)
-        def _():
-            own_part()
-
-        @pl.when(s == step_f)
-        def _():
-            @pl.when(c > 0)
-            def _():
-                received(f_in, "f")
-                f_out[...] = dot3(f_in[...], th[...], tl[...]) + o_buf[...]
-
-            @pl.when(c < LAST)
-            def _():
-                copy(*next_f()).start()
-
-            @pl.when(both(c == LAST, r > 0, r < rows - 1))
-            def _():
-                copy(*row_offset()).start()
-
-            @pl.when(both(c == LAST, r == 0, r < rows - 1))
-            def _():
-                copy(*first_offset()).start()
-                copy(*first_far()).start()
-
-        @pl.when(both(s > 2, s < 5))
-        def _():
-            k = s - 3
+        @pl.when(both(s > 5, s < 8))
+        def _():
+            k = s - 6
             for t in range(tiles):
                 lanes = slice(t * LANES, (t + 1) * LANES)
                 dth[k, :, lanes] = jnp.transpose(dh[k, lanes, :])
                 dtl[k, :, lanes] = jnp.transpose(dl[k, lanes, :])
 
-        @pl.when(both(c == HUB, s > middle - tiles, s <= middle))
+        @pl.when(both(c == HUB, has_a, has_s, s > middle - tiles, s <= middle))
         def _():
             i = s - (middle - tiles + 1)
             some = pl.ds(pl.multiple_of(i * LANES, LANES), LANES)
@@ -407,23 +453,33 @@
         return 0
 
     lax.fori_loop(0, (ROW // 2 - 1) * 4 + 1 + BLOCKS, slot, 0)
-    waits.append((lambda: c < LAST, next_f))
-    waits.append((lambda: both(c == LAST, r > 0, r < rows - 1), row_offset))
-    waits.append((lambda: both(c == LAST, r == 0, r < rows - 1), first_offset))
-    waits.append((lambda: both(c == LAST, r == 0, r < rows - 1), first_far))
-
-    def spread(cond, buf, name):
+    for part in range(2):
+        waits.append((lambda: c < LAST, functools.partial(next_f, part)))
+        waits.append(
+            (lambda: both(c == LAST, r > 0, r < rows - 1), functools.partial(row_offset, part))
+        )
+        for late in (first_offset, first_far):
+            waits.append(
+                (lambda: both(c == LAST, r == 0, r < rows - 1), functools.partial(late, part))
+            )
+
+    def spread(cond, buf, name, part):
         @pl.when(c == HUB)
         def _():
             for spoke in (1, 5, HUB - 1):
                 send(
                     lambda: both(cond(), c == HUB),
-                    lambda spoke=spoke: (buf, buf, name + str(spoke), name, base + spoke),
+                    lambda spoke=spoke: (
+                        buf, buf, name + str(spoke), name, base + spoke, None, part,
+                    ),
                 )
 
         @pl.when(is_spoke)
         def _():
-            send(lambda: both(cond(), is_spoke), lambda: (buf, buf, name + "_pair", name, d - 1))
+            send(
+                lambda: both(cond(), is_spoke),
+                lambda: (buf, buf, name + "_pair", name, d - 1, None, part),
+            )
 
     @pl.when(r == 0)
     def _():
@@ -431,17 +487,30 @@
 
     @pl.when(r > 0)
     def _():
-        received(eb, "down")
-        spread(lambda: r > 0, eb, "down")
-
-        @pl.when(both(c == HUB, r < rows - 1))
-        def _():
-            received(o_down, "o")
-            e_next[...] = dot3(eb[...], mh[...], ml[...], True) + o_down[...]
-            for name, to in (("down_hub", HUB), ("down_far", LAST)):
+        for part in range(2):
+            some = half(part)
+            received(eb, "down", part)
+            spread(lambda: r > 0, eb, "down", part)
+
+            @pl.when(both(c == HUB, r < rows - 1))
+            def _():
+                received(o_down, "o", part)
+                e_next[some] = dot3(eb[some], mh[...], ml[...], True) + o_down[some]
                 send(
                     lambda: both(c == HUB, r > 0, r < rows - 1),
-                    lambda name=name, to=to: (e_next, eb, name, "down", base + ROW + to),
+                    lambda part=part: (
+                        e_next, eb, "down_hub", "down", base + ROW + HUB, None, part,
+                    ),
+                )
+
+        @pl.when(both(c == HUB, r < rows - 1))
+        def _():
+            for part in range(2):
+                send(
+                    lambda: both(c == HUB, r > 0, r < rows - 1),
+                    lambda part=part: (
+                        e_next, eb, "down_far", "down", base + ROW + LAST, None, part,
+                    ),
                 )
 
         @pl.when(c == 0)
@@ -461,8 +530,8 @@
     halo_received(ylo, yhi, "y")
     add_neighbours(h, ylo, yhi)
 
-    def next_g():
-        return g_out, g_in, "g_prev", "g", d - 1
+    def next_g(part):
+        return g_out, g_in, "g_prev", "g", d - 1, None, part
 
     above = dot3(h[1], dth[1], dtl[1])
     p_buf[...] = vert[0:1, :] * dot3(h[0] + vert[1:2, :] * above, dth[0], dtl[0])
@@ -471,7 +540,8 @@
     def _():
         g_in[...] = jnp.zeros(g_in.shape, F32)
         g_out[...] = p_buf[...]
-        copy(*next_g()).start()
+        for part in range(2):
+            copy(*next_g(part)).start()
 
     @pl.when(r > 0)
     def _():
@@ -483,64 +553,81 @@
         def _():
             w_out[...] = dot3(p_buf[...], ah[...], al[...], True)
 
-        @pl.when(c % 2 == 0)
+        @pl.when(c == HUB - 1)
         def _():
             send(
-                lambda: both(r > 0, c % 2 == 0),
+                lambda: both(r > 0, c == HUB - 1),
                 lambda: (w_out, w_pair, "w_pair", "w_pair", d + 1),
             )
 
-        @pl.when(c % 2 == 1)
-        def _():
-            received(w_pair, "w_pair")
-            w_out[...] = w_out[...] + w_pair[...]
-
-        for i, spoke in enumerate(SPOKES):
-
-            @pl.when(c == spoke)
+        for i, other in enumerate(SPOKES + OUTER):
+
+            @pl.when(c == other)
             def _():
                 send(
-                    lambda spoke=spoke: both(r > 0, c == spoke),
+                    lambda other=other: both(r > 0, c == other),
                     lambda i=i: (w_out, w_hub.at[i], "w_hub", "w" + str(i), base + HUB),
                 )
 
         @pl.when(c == HUB)
         def _():
-            for spoke in range(3):
-                received(w_hub.at[spoke], "w" + str(spoke))
-            o_up[...] = w_out[...] + (w_hub[0] + (w_hub[1] + w_hub[2]))
+            received(w_pair, "w_pair")
+            own = w_out[...] + w_pair[...]
+            for other in range(len(SPOKES + OUTER)):
+                received(w_hub.at[other], "w" + str(other))
+                own = own + w_hub[other]
+            o_up[...] = own
 
             @pl.when(r == rows - 1)
             def _():
                 for name, to in (("up_hub", HUB), ("up_far", LAST)):
-                    send(
-                        lambda: both(c == HUB, r > 0, r == rows - 1),
-                        lambda name=name, to=to: (o_up, ub, name, "up", base - ROW + to),
-                    )
+                    for part in range(2):
+                        send(
+                            lambda: both(c == HUB, r > 0, r == rows - 1),
+                            lambda name=name, to=to, part=part: (
+                                o_up, ub, name, "up", base - ROW + to, None, part,
+                            ),
+                        )
 
     @pl.when(c < LAST)
     def _():
-        received(g_in, "g")
-
-        @pl.when(c > 0)
-        def _():
-            g_out[...] = dot3(g_in[...], tth[...], ttl[...]) + p_buf[...]
-            copy(*next_g()).start()
-
-    waits.append((lambda: c > 0, next_g))
+        for part in range(2):
+            some = half(part)
+            received(g_in, "g", part)
+
+            @pl.when(c > 0)
+            def _():
+                g_out[some] = dot3(g_in[some], tth[...], ttl[...]) + p_buf[some]
+                copy(*next_g(part)).start()
+
+    for part in range(2):
+        waits.append((lambda: c > 0, functools.partial(next_g, part)))
 
     @pl.when(r < rows - 1)
     def _():
-        received(ub, "up")
-        spread(lambda: r < rows - 1, ub, "up")
-
-        @pl.when(both(c == HUB, r > 0))
-        def _():
-            u_next[...] = dot3(ub[...], mh[...], ml[...]) + o_up[...]
-            for name, to in (("up_hub", HUB), ("up_far", LAST)):
+        for part in range(2):
+            some = half(part)
+            received(ub, "up", part)
+            spread(lambda: r < rows - 1, ub, "up", part)
+
+            @pl.when(both(c == HUB, r > 0))
+            def _():
+                u_next[some] = dot3(ub[some], mh[...], ml[...]) + o_up[some]
                 send(
                     lambda: both(c == HUB, r > 0, r < rows - 1),
-                    lambda name=name, to=to: (u_next, ub, name, "up", base - ROW + to),
+                    lambda part=part: (
+                        u_next, ub, "up_hub", "up", base - ROW + HUB, None, part,
+                    ),
+                )
+
+        @pl.when(both(c == HUB, r > 0))
+        def _():
+            for part in range(2):
+                send(
+                    lambda: both(c == HUB, r > 0, r < rows - 1),
+                    lambda part=part: (
+                        u_next, ub, "up_far", "up", base - ROW + LAST, None, part,
+                    ),
                 )
 
         @pl.when(c == LAST)
@@ -560,12 +647,12 @@
         def _():
             copy(*args()).wait_send()
 
-    @pl.when(c < LAST)
+    @pl.when(both(c < LAST, has_a))
     def _():
         for b in range(BLOCKS):
             block_a(b).wait_send()
 
-    @pl.when(c > 0)
+    @pl.when(both(c > 0, has_s))
     def _():
         for b in range(BLOCKS):
             block_s(b).wait_send()
@@ -604,12 +691,12 @@
         + [state] * 3
         + [pltpu.VMEM(field, F32)] * 2
         + [state] * 3
-        + [pltpu.VMEM((3, count, width), F32)] + [state]
+        + [pltpu.VMEM((6, count, width), F32)] + [state]
         + [state] * 4
         + [
             pltpu.SemaphoreType.DMA((4,)),
-            pltpu.SemaphoreType.DMA((len(SENDS),)),
-            pltpu.SemaphoreType.DMA((len(RECVS),)),
+            pltpu.SemaphoreType.DMA((len(SENDS), 2)),
+            pltpu.SemaphoreType.DMA((len(RECVS), 2)),
         ]
         + [pltpu.SemaphoreType.DMA((BLOCKS,))] * 4
     )

time: 63 us -> 61.3 us (0.973)
  the two profiles are of different devices: /device:TPU:224 before, /device:TPU:192 now
where the time goes in v3:
time: 61.3 us; the launch traced here: 61.1 us
  Pallas kernels  60.4 us (99%)
  local copies, waits for them, and re-layouts  0.66 us (1%)
    pallas_call x1, Pallas kernels, shards(): pl.pallas_call(functools.partial(kernel, depth, areas), out_shape=pltpu.V...  60.4 us

profile of v3, /device:TPU:192, one launch (start us, length us, event | category | flops | bytes accessed | tf_op | source)
XLA Modules:
  0.0 61.1 jit_solution(16525526583475907557)
XLA Ops:
  0.0 60.4 %sweep.1 = f32[2,32,512]{2,1,0:T(8,128)S(1)} custom-call(f32[4,8]{1,0:T(4,128)} %bitcast.3, f32[8]{0:T(128)} %vert_tab.1, s32[2,512]{1,0:T(2,128)} %facies.1, s32[4,512]{1,0:T(4,128)} %bitcast.2, f32[2,32,512]{2,1,0:T(8,128)} %rhs_hbm.1, f32[2,32,512]{2,1,0:T(8,128)} %start_hbm.1, f32[2,512,512]{2,1,0:T(8,128)} %inv_hbm.1), custom_call_target="tpu_custom_call" | custom-call | tf_op jit(solution)/shard_map/sweep/pallas_call | solution.py:706
  60.4 0.7 %copy.9 = f32[2,32,512]{2,1,0:T(8,128)} copy(f32[2,32,512]{2,1,0:T(8,128)S(1)} %sweep.1) | data formatting | bytes 262144

commit v4 on v3

--- a/solution.py
+++ b/solution.py
@@ -20,13 +20,13 @@
 BLOCKS = 8
 
 SENDS = (
-    "start_right", "start_left", "below", "f_next", "o_hub", "down_hub",
+    "start_right", "start_left", "below", "f_next", "q_next", "q_far", "q_relay", "down_hub",
     "down_far", "down1", "down5", "down2", "down_pair", "y_right",
     "y_left", "w_pair", "w_hub", "g_prev", "up_hub", "up_far",
     "up1", "up5", "up2", "up_pair",
 )
 RECVS = (
-    "start_lo", "start_hi", "below", "f", "o", "down",
+    "start_lo", "start_hi", "below", "f", "q", "o", "down",
     "y_lo", "y_hi", "w_pair", "w0", "w1", "w2",
     "w3", "w4", "w5", "g", "up",
 )
@@ -57,7 +57,7 @@
     out,
     rhs, start, inv, dh, dl, dth, dtl, th, tl, tth, ttl, ina, ah, al, outa, ins, sh, sl, outs, bh, bl, mh, ml,
     lat_h, lat_l, wts, wsum, vert, slo, shi, ylo, yhi, to_right, to_left, below_out, below_in,
-    g, f_in, f_out, o_buf, o_down, eb, e_next, e_in, y, h, p_buf, w_out, w_pair, w_hub, o_up,
+    g, f_in, f_out, o_buf, o_down, q_in, q_out, eb, e_next, e_in, y, h, p_buf, w_out, w_pair, w_hub, o_up,
     g_in, g_out, ub, u_next,
     local, snd, rcv, snd_a, rcv_a, snd_s, rcv_s,
 ):
@@ -114,11 +114,18 @@
     loads = [
         pltpu.make_async_copy(start_hbm, start, local.at[0]),
         pltpu.make_async_copy(inv_hbm.at[1], inv.at[1], local.at[1]),
-        pltpu.make_async_copy(inv_hbm.at[0], inv.at[0], local.at[2]),
-        pltpu.make_async_copy(rhs_hbm, rhs, local.at[3]),
+        pltpu.make_async_copy(rhs_hbm, rhs, local.at[2]),
     ]
-    for load in loads:
-        load.start()
+
+    def load_rows(i):
+        some = pl.ds(pl.multiple_of(i * LANES, LANES), LANES)
+        return pltpu.make_async_copy(inv_hbm.at[0, some], inv.at[0, some], local.at[3 + i])
+
+    loads[0].start()
+    loads[1].start()
+    for i in range(tiles):
+        load_rows(i).start()
+    loads[2].start()
 
     barrier = pltpu.get_barrier_semaphore()
     is_spoke = both(c % 2 == 1, c != HUB)
@@ -136,6 +143,8 @@
         (both(c == LAST, r < rows - 1), d + ROW - (LAST - HUB), z),
         (both(c == LAST, r == 0, r < rows - 1), d + ROW, z),
         (both(c == LAST, r == 1), d - ROW, z),
+        (c == LAST, base + 1, z),
+        (c == 1, base + LAST, z),
         (both(c % 2 == 0, c != HUB - 1), base + HUB, z),
     ] + [(c == HUB, base + other, z) for other in SPOKES + OUTER]
     for cond, to_depth, to_area in partners:
@@ -268,6 +277,7 @@
         return inv[0, some, :] * vert[1:2, :] * jnp.concatenate([scale] * tiles, axis=1)
 
     def compose(i, _):
+        load_rows(i).wait()
         some = pl.ds(pl.multiple_of(i * LANES, LANES), LANES)
         product = dot3(scaled_rows(some), dh[1], dl[1])
         high, low = split(product)
@@ -290,6 +300,7 @@
         return 0
 
     def halves_of_left(i, _):
+        load_rows(i).wait()
         some = pl.ds(pl.multiple_of(i * LANES, LANES), LANES)
         high, low = split(scaled_rows(some))
         sh[some, :] = high
@@ -311,7 +322,6 @@
 
     starts_s = both(c == LAST, has_s)
     loads[1].wait()
-    loads[2].wait()
 
     @pl.when(starts_s)
     def _():
@@ -323,12 +333,10 @@
     def _():
         split_layer(1)
         lax.fori_loop(0, tiles, compose, 0)
-        lax.fori_loop(0, tiles, turn, 0)
-
-    split_layer(0)
 
     def own_part():
-        loads[3].wait()
+        split_layer(0)
+        loads[2].wait()
         g[0] = rhs[0] - lateral_own(0, start[0]) + vert[1:2, :] * start[1]
         g[1] = rhs[1] - lateral_own(1, start[1])
         halo_received(slo, shi, "start")
@@ -350,13 +358,18 @@
     step_a = (c // 2) * 4 + c % 2
     last = LAST - c
     step_s = (last // 2) * 4 + last % 2
-    middle = (HUB // 2) * 4 + 4 + BLOCKS - 1
 
     def next_f(part):
         return f_out, f_in, "f_next", "f", d + 1, None, part
 
-    def row_offset(part):
-        return f_out, o_down, "o_hub", "o", base + HUB, None, part
+    def next_q():
+        return q_out, q_in, "q_next", "q", d + 1
+
+    def far_q():
+        return q_out, q_in, "q_far", "q", base + 1
+
+    def relay_q():
+        return q_in, o_down, "q_relay", "o", base + HUB
 
     def first_offset(part):
         return f_out, eb, "down_hub", "down", base + ROW + HUB, None, part
@@ -365,6 +378,8 @@
         return f_out, eb, "down_far", "down", base + ROW + LAST, None, part
 
     step_f = jnp.where(has_a, jnp.maximum(step_a + 1, 2), jnp.maximum(step_a, 1))
+    has_q = both(has_a, has_s)
+    step_q = jnp.where(c == HUB + 1, 3, jnp.where(c == HUB + 2, 4, jnp.where(c == 1, 11, c + 3)))
     step_own = jnp.where(has_a, jnp.where(c <= 1, 2, 3), 1)
 
     def slot(s, _):
@@ -407,10 +422,6 @@
                 def _():
                     copy(*next_f(part)).start()
 
-                @pl.when(both(c == LAST, r > 0, r < rows - 1))
-                def _():
-                    copy(*row_offset(part)).start()
-
                 @pl.when(both(c == LAST, r == 0, r < rows - 1))
                 def _():
                     copy(*first_offset(part)).start()
@@ -419,6 +430,34 @@
             def _():
                 for part in range(2):
                     copy(*first_far(part)).start()
+
+        @pl.when(both(has_q, s == step_q))
+        def _():
+            @pl.when(c == HUB + 1)
+            def _():
+                q_out[...] = o_buf[...]
+
+            @pl.when(c > HUB + 1)
+            def _():
+                received(q_in, "q")
+                q_out[...] = dot3(q_in[...], th[...], tl[...]) + o_buf[...]
+
+            @pl.when(both(c > HUB, c < LAST))
+            def _():
+                copy(*next_q()).start()
+
+            @pl.when(c == LAST)
+            def _():
+                copy(*far_q()).start()
+
+            @pl.when(c == 1)
+            def _():
+                received(q_in, "q")
+                copy(*relay_q()).start()
+
+        @pl.when(both(s == 4, jnp.logical_not(starts_s)))
+        def _():
+            lax.fori_loop(0, tiles, turn, 0)
 
         @pl.when(both(c < LAST, has_s, s >= step_s, s < step_s + BLOCKS))
         def _():
@@ -429,7 +468,12 @@
             sh[some, :] = high
             sl[some, :] = low
 
-            @pl.when(c > 0)
+            @pl.when(c == LAST - 1)
+            def _():
+                outs[b] = dot_halves(high, low, th[...], tl[...], True)
+                block_s(b).start()
+
+            @pl.when(both(c > 0, c < LAST - 1))
             def _():
                 outs[b] = dot_halves(high, low, tth[...], ttl[...], False)
                 block_s(b).start()
@@ -442,22 +486,14 @@
                 dth[k, :, lanes] = jnp.transpose(dh[k, lanes, :])
                 dtl[k, :, lanes] = jnp.transpose(dl[k, lanes, :])
 
-        @pl.when(both(c == HUB, has_a, has_s, s > middle - tiles, s <= middle))
-        def _():
-            i = s - (middle - tiles + 1)
-            some = pl.ds(pl.multiple_of(i * LANES, LANES), LANES)
-            high, low = split(dot_halves(sh[some, :], sl[some, :], bh[...], bl[...], True))
-            mh[some, :] = high
-            ml[some, :] = low
-
         return 0
 
     lax.fori_loop(0, (ROW // 2 - 1) * 4 + 1 + BLOCKS, slot, 0)
+    waits.append((lambda: both(has_q, c > HUB, c < LAST), next_q))
+    waits.append((lambda: both(has_q, c == LAST), far_q))
+    waits.append((lambda: both(has_q, c == 1), relay_q))
     for part in range(2):
         waits.append((lambda: c < LAST, functools.partial(next_f, part)))
-        waits.append(
-            (lambda: both(c == LAST, r > 0, r < rows - 1), functools.partial(row_offset, part))
-        )
         for late in (first_offset, first_far):
             waits.append(
                 (lambda: both(c == LAST, r == 0, r < rows - 1), functools.partial(late, part))
@@ -487,6 +523,10 @@
 
     @pl.when(r > 0)
     def _():
+        @pl.when(both(c == HUB, r < rows - 1))
+        def _():
+            received(o_down, "o")
+
         for part in range(2):
             some = half(part)
             received(eb, "down", part)
@@ -494,8 +534,8 @@
 
             @pl.when(both(c == HUB, r < rows - 1))
             def _():
-                received(o_down, "o", part)
-                e_next[some] = dot3(eb[some], mh[...], ml[...], True) + o_down[some]
+                across = dot3(eb[some], bh[...], bl[...]) + f_out[some]
+                e_next[some] = dot3(across, sh[...], sl[...], True) + o_down[some]
                 send(
                     lambda: both(c == HUB, r > 0, r < rows - 1),
                     lambda part=part: (
@@ -512,6 +552,15 @@
                         e_next, eb, "down_far", "down", base + ROW + LAST, None, part,
                     ),
                 )
+
+            def product(i, _):
+                some = pl.ds(pl.multiple_of(i * LANES, LANES), LANES)
+                high, low = split(dot_halves(sh[some, :], sl[some, :], bh[...], bl[...], True))
+                mh[some, :] = high
+                ml[some, :] = low
+                return 0
+
+            lax.fori_loop(0, tiles, product, 0)
 
         @pl.when(c == 0)
         def _():
@@ -687,14 +736,14 @@
         + [halo] * 4
         + [pltpu.VMEM((2, count, LANES), F32)] * 2
         + [state] * 2
-        + [pltpu.VMEM(field, F32)] + [state] * 4
+        + [pltpu.VMEM(field, F32)] + [state] * 6
         + [state] * 3
         + [pltpu.VMEM(field, F32)] * 2
         + [state] * 3
         + [pltpu.VMEM((6, count, width), F32)] + [state]
         + [state] * 4
         + [
-            pltpu.SemaphoreType.DMA((4,)),
+            pltpu.SemaphoreType.DMA((3 + tiles,)),
             pltpu.SemaphoreType.DMA((len(SENDS), 2)),
             pltpu.SemaphoreType.DMA((len(RECVS), 2)),
         ]

time: 61.3 us -> 60.8 us (level)
  the two profiles are of different devices: /device:TPU:192 before, /device:TPU:64 now
where the time goes in v4:
time: 60.8 us; the launch traced here: 60.6 us
  Pallas kernels  59.9 us (99%)
  local copies, waits for them, and re-layouts  0.66 us (1%)
    pallas_call x1, Pallas kernels, shards(): pl.pallas_call(functools.partial(kernel, depth, areas), out_shape=pltpu.V...  59.9 us

profile of v4, /device:TPU:64, one launch (start us, length us, event | category | flops | bytes accessed | tf_op | source)
XLA Modules:
  0.0 60.6 jit_solution(2011963862355768852)
XLA Ops:
  0.0 59.9 %sweep.1 = f32[2,32,512]{2,1,0:T(8,128)S(1)} custom-call(f32[4,8]{1,0:T(4,128)} %bitcast.3, f32[8]{0:T(128)} %vert_tab.1, s32[2,512]{1,0:T(2,128)} %facies.1, s32[4,512]{1,0:T(4,128)} %bitcast.2, f32[2,32,512]{2,1,0:T(8,128)} %rhs_hbm.1, f32[2,32,512]{2,1,0:T(8,128)} %start_hbm.1, f32[2,512,512]{2,1,0:T(8,128)} %inv_hbm.1), custom_call_target="tpu_custom_call" | custom-call | tf_op jit(solution)/shard_map/sweep/pallas_call | solution.py:755
  60.0 0.7 %copy.9 = f32[2,32,512]{2,1,0:T(8,128)} copy(f32[2,32,512]{2,1,0:T(8,128)S(1)} %sweep.1) | data formatting | bytes 262144

commit v5 on v4

--- a/solution.py
+++ b/solution.py
@@ -53,9 +53,9 @@
 
 def kernel(
     depth, areas,
-    lat_tab, vert_tab, facies, nbrs, rhs_hbm, start_hbm, inv_hbm,
+    lat_tab_hbm, vert_tab_hbm, facies_hbm, nbrs_hbm, rhs_hbm, start_hbm, inv_hbm,
     out,
-    rhs, start, inv, dh, dl, dth, dtl, th, tl, tth, ttl, ina, ah, al, outa, ins, sh, sl, outs, bh, bl, mh, ml,
+    lat_tab, vert_tab, facies, nbrs, rhs, start, inv, dh, dl, dth, dtl, th, tl, tth, ttl, ina, ah, al, outa, ins, sh, sl, outs, bh, bl, mh, ml,
     lat_h, lat_l, wts, wsum, vert, slo, shi, ylo, yhi, to_right, to_left, below_out, below_in,
     g, f_in, f_out, o_buf, o_down, q_in, q_out, eb, e_next, e_in, y, h, p_buf, w_out, w_pair, w_hub, o_up,
     g_in, g_out, ub, u_next,
@@ -121,6 +121,14 @@
         some = pl.ds(pl.multiple_of(i * LANES, LANES), LANES)
         return pltpu.make_async_copy(inv_hbm.at[0, some], inv.at[0, some], local.at[3 + i])
 
+    small = [
+        pltpu.make_async_copy(source, target, local.at[3 + tiles + i])
+        for i, (source, target) in enumerate(
+            ((facies_hbm, facies), (nbrs_hbm, nbrs), (lat_tab_hbm, lat_tab), (vert_tab_hbm, vert_tab))
+        )
+    ]
+    for load in small:
+        load.start()
     loads[0].start()
     loads[1].start()
     for i in range(tiles):
@@ -155,6 +163,8 @@
                 barrier, inc=1, device_id=(to_depth, to_area), device_id_type=MESH
             )
 
+    for load in small:
+        load.wait()
     kinds = facies[...]
     facies_count = lat_tab.shape[1]
     v_rows = jnp.zeros(kinds.shape, F32)
@@ -723,7 +733,9 @@
 
     halo = pltpu.VMEM((count, LANES), F32)
     scratch = (
-        [pltpu.VMEM(field, F32)] * 2
+        [pltpu.SMEM(lateral_table.shape[::-1], F32), pltpu.SMEM(vertical_table.shape, F32)]
+        + [pltpu.VMEM(facies.shape, jnp.int32), pltpu.VMEM(neighbours.shape[::-1], jnp.int32)]
+        + [pltpu.VMEM(field, F32)] * 2
         + [pltpu.VMEM((layers,) + matrix, F32)]
         + [pltpu.VMEM((layers,) + matrix, BF16)] * 4
         + halves() * 2
@@ -743,19 +755,18 @@
         + [pltpu.VMEM((6, count, width), F32)] + [state]
         + [state] * 4
         + [
-            pltpu.SemaphoreType.DMA((3 + tiles,)),
+            pltpu.SemaphoreType.DMA((7 + tiles,)),
             pltpu.SemaphoreType.DMA((len(SENDS), 2)),
             pltpu.SemaphoreType.DMA((len(RECVS), 2)),
         ]
         + [pltpu.SemaphoreType.DMA((BLOCKS,))] * 4
     )
     vmem = pl.BlockSpec(memory_space=pltpu.VMEM)
-    smem = pl.BlockSpec(memory_space=pltpu.SMEM)
     hbm = pl.BlockSpec(memory_space=pl.ANY)
     return pl.pallas_call(
         functools.partial(kernel, depth, areas),
         out_shape=pltpu.VMEM(field, F32),
-        in_specs=[smem, smem, vmem, vmem, hbm, hbm, hbm],
+        in_specs=[hbm] * 7,
         out_specs=vmem,
         scratch_shapes=scratch,
         compiler_params=pltpu.CompilerParams(

time: 60.8 us -> 60.1 us (0.988)
    pallas_call x1, Pallas kernels: 59.9 us -> 59.3 us  [shards(): pl.pallas_call(functools.partial(kernel, depth, areas), out_shape=pltpu.V...]
where the time goes in v5:
time: 60.1 us; the launch traced here: 59.9 us
  Pallas kernels  59.3 us (99%)
  local copies, waits for them, and re-layouts  0.66 us (1%)
    pallas_call x1, Pallas kernels, shards(): pl.pallas_call(functools.partial(kernel, depth, areas), out_shape=pltpu.V...  59.3 us

profile of v5, /device:TPU:64, one launch (start us, length us, event | category | flops | bytes accessed | tf_op | source)
XLA Modules:
  0.0 59.9 jit_solution(18047673480003247462)
XLA Ops:
  0.0 59.3 %sweep.1 = f32[2,32,512]{2,1,0:T(8,128)S(1)} custom-call(f32[4,8]{1,0:T(4,128)} %bitcast.3, f32[8]{0:T(128)} %vert_tab_hbm.1, s32[2,512]{1,0:T(2,128)} %facies_hbm.1, s32[4,512]{1,0:T(4,128)} %bitcast.2, f32[2,32,512]{2,1,0:T(8,128)} %rhs_hbm.1, f32[2,32,512]{2,1,0:T(8,128)} %start_hbm.1, f32[2,512,512]{2,1,0:T(8,128)} %inv_hbm.1), custom_call_target="tpu_custom_call" | custom-call | tf_op jit(solution)/shard_map/sweep/pallas_call | solution.py:766
  59.3 0.7 %copy.9 = f32[2,32,512]{2,1,0:T(8,128)} copy(f32[2,32,512]{2,1,0:T(8,128)S(1)} %sweep.1) | data formatting | bytes 262144

commit v6 on v5

--- a/solution.py
+++ b/solution.py
@@ -55,7 +55,7 @@
     depth, areas,
     lat_tab_hbm, vert_tab_hbm, facies_hbm, nbrs_hbm, rhs_hbm, start_hbm, inv_hbm,
     out,
-    lat_tab, vert_tab, facies, nbrs, rhs, start, inv, dh, dl, dth, dtl, th, tl, tth, ttl, ina, ah, al, outa, ins, sh, sl, outs, bh, bl, mh, ml,
+    lat_tab, vert_tab, facies, nbrs, rhs, start, inv, dh, dl, dth, dtl, th, tl, tth, ttl, ina, ah, al, aht, alt, outa, ins, sh, sl, outs, bh, bl, mh, ml,
     lat_h, lat_l, wts, wsum, vert, slo, shi, ylo, yhi, to_right, to_left, below_out, below_in,
     g, f_in, f_out, o_buf, o_down, q_in, q_out, eb, e_next, e_in, y, h, p_buf, w_out, w_pair, w_hub, o_up,
     g_in, g_out, ub, u_next,
@@ -586,6 +586,14 @@
     halo(y, ylo, yhi, "y", 1)
     h[0] = rhs[0] - lateral_own(0, y[0]) + entering
     h[1] = rhs[1] - lateral_own(1, y[1]) + vert[1:2, :] * y[0]
+
+    @pl.when(both(c > 0, r > 0))
+    def _():
+        for t in range(tiles):
+            lanes = slice(t * LANES, (t + 1) * LANES)
+            aht[:, lanes] = jnp.transpose(ah[lanes, :])
+            alt[:, lanes] = jnp.transpose(al[lanes, :])
+
     halo_received(ylo, yhi, "y")
     add_neighbours(h, ylo, yhi)
 
@@ -610,7 +618,7 @@
 
         @pl.when(c > 0)
         def _():
-            w_out[...] = dot3(p_buf[...], ah[...], al[...], True)
+            w_out[...] = dot3(p_buf[...], aht[...], alt[...])
 
         @pl.when(c == HUB - 1)
         def _():
@@ -739,7 +747,7 @@
         + [pltpu.VMEM((layers,) + matrix, F32)]
         + [pltpu.VMEM((layers,) + matrix, BF16)] * 4
         + halves() * 2
-        + [blocks()] + halves() + [blocks()]
+        + [blocks()] + halves() * 2 + [blocks()]
         + [blocks()] + halves() + [blocks()]
         + halves() * 2
         + [pltpu.VMEM((layers, tiles, 3 * LANES, LANES), BF16)] * 2

time: 60.1 us -> 59.9 us (level)
  no operation moved by 1% of the time
where the time goes in v6:
time: 59.9 us; the launch traced here: 59.8 us
  Pallas kernels  59.1 us (99%)
  local copies, waits for them, and re-layouts  0.66 us (1%)
    pallas_call x1, Pallas kernels, shards(): pl.pallas_call(functools.partial(kernel, depth, areas), out_shape=pltpu.V...  59.1 us

profile of v6, /device:TPU:64, one launch (start us, length us, event | category | flops | bytes accessed | tf_op | source)
XLA Modules:
  0.0 59.8 jit_solution(1392524074060846597)
XLA Ops:
  0.0 59.1 %sweep.1 = f32[2,32,512]{2,1,0:T(8,128)S(1)} custom-call(f32[4,8]{1,0:T(4,128)} %bitcast.3, f32[8]{0:T(128)} %vert_tab_hbm.1, s32[2,512]{1,0:T(2,128)} %facies_hbm.1, s32[4,512]{1,0:T(4,128)} %bitcast.2, f32[2,32,512]{2,1,0:T(8,128)} %rhs_hbm.1, f32[2,32,512]{2,1,0:T(8,128)} %start_hbm.1, f32[2,512,512]{2,1,0:T(8,128)} %inv_hbm.1), custom_call_target="tpu_custom_call" | custom-call | tf_op jit(solution)/shard_map/sweep/pallas_call | solution.py:774
  59.1 0.7 %copy.9 = f32[2,32,512]{2,1,0:T(8,128)} copy(f32[2,32,512]{2,1,0:T(8,128)S(1)} %sweep.1) | data formatting | bytes 262144
